TPU v7x, 16 devices: a whole 2x2x2 slice. The times are simulated.
16 devices in a mesh: frag: 4 (over z, y), dev: 4 (over x, core).
Axes of the slice: x: 2, y: 2, z: 2, core: 2. Of those that a mesh axis runs over, the one named last changes fastest.
Arguments:
- a_ints: bfloat16 [448, 112, 112, 112], P(('frag', 'dev')), parts along dimension 0
- c_occ: bfloat16 [448, 64], P('frag'), parts along dimension 0
- c_vir: bfloat16 [448, 32], P('frag'), parts along dimension 0
- eps_occ: float32 [256], P('frag'), parts along dimension 0
- eps_vir: float32 [128], P('frag'), parts along dimension 0
Outputs:
- output: float32 [256, 64], P('frag', 'dev'), parts along dimension 0
There are 4 independent parts. A program takes and returns all parts, laid end to end along the dimension named above; each array names one.
All inputs are finite; a program needn't handle non-finite values.
Results may differ from a plain program's by a relative error of at most 0.001.
Values are sent between devices in bfloat16 or wider.
A program may use at most 1 GiB of HBM per device.

v0:
```python
import jax
import jax.numpy as jnp
from jax import lax
from jax.sharding import PartitionSpec as P, NamedSharding


def pair_energies(v_mo, eps_j, eps_occ, eps_vir):
    v_swap = jnp.swapaxes(v_mo, 1, 2)
    denominator = (eps_j[:, None, None, None] + eps_occ[None, None, None, :]
                   - eps_vir[None, :, None, None] - eps_vir[None, None, :, None])
    pair_ji = jnp.sum(v_mo * (2.0 * v_mo - v_swap) / denominator, axis=(1, 2))
    return pair_ji.T


def solution(mesh):
    group_size = mesh.shape["dev"]

    def per_device(a_ints, c_occ, c_vir, eps_occ, eps_vir):
        occ_dev = c_occ.shape[1] // group_size
        t_one = jnp.einsum("pqrs,rj->pqsj", a_ints, c_occ, preferred_element_type=jnp.float32).astype(jnp.bfloat16)
        half_mo = jnp.einsum("pqsj,sb->pqjb", t_one, c_vir, preferred_element_type=jnp.float32).astype(jnp.bfloat16)
        half_mo = lax.all_to_all(half_mo, "dev", 2, 0, tiled=True)
        g_mat = jnp.einsum("pqjb,qa->pjba", half_mo, c_vir, preferred_element_type=jnp.float32).astype(jnp.bfloat16)
        v_mo = jnp.einsum("pjba,pi->jbai", g_mat, c_occ, preferred_element_type=jnp.float32)
        eps_j = lax.dynamic_slice_in_dim(eps_occ, lax.axis_index("dev") * occ_dev, occ_dev)
        return pair_energies(v_mo, eps_j, eps_occ, eps_vir)

    return jax.shard_map(
        per_device,
        mesh=mesh,
        in_specs=(P(("frag", "dev")), P("frag"), P("frag"), P("frag"), P("frag")),
        out_specs=P("frag", "dev"),
        check_vma=False,
    )
```

profile of v0, /device:TPU:0, one launch (start us, length us, event | category | flops | bytes accessed | tf_op | source)
XLA Modules:
  0.0 376.2 jit_solution(9468671941544046262)
XLA Ops:
  0.0 0.0 copy-start
  0.0 0.0 copy-start.1
  0.0 0.7 copy-done
  0.7 47.8 %convolution_convert_fusion = bf16[28,112,112,64]{2,3,1,0:T(8,128)(2,1)} fusion(bf16[28,112,112,112]{3,2,1,0:T(8,128)(2,1)} %param.5, bf16[112,64]{0,1:T(8,128)(2,1)S(1)} %copy-done), kind=kOutput, calls=%fused_computation.2 | convolution fusion | flops 5057740800 | bytes 123648000 | tf_op jit(solution)/shard_map/pqrs,rj->pqsj/dot_general | solution.py:20
  48.5 0.0 copy-done.1
  48.5 88.8 %fusion.4 = bf16[28,112,64,32]{1,3,2,0:T(8,128)(2,1)} fusion(bf16[28,112,112,64]{2,3,1,0:T(8,128)(2,1)} %convolution_convert_fusion, bf16[112,32]{0,1:T(8,128)(2,1)S(1)} %copy-done.1), kind=kOutput, calls=%fused_computation.5 | convolution fusion | flops 1445068800 | bytes 57809920 | tf_op jit(solution)/shard_map/pqsj,sb->pqjb/dot_general | solution.py:21
  137.3 14.9 %copy.14 = bf16[28,112,64,32]{1,3,0,2:T(8,128)(2,1)} copy(bf16[28,112,64,32]{1,3,2,0:T(8,128)(2,1)} %fusion.4) | data formatting | bytes 25690112 | tf_op jit(solution)/shard_map/convert_element_type | solution.py:21
  152.2 0.0 copy-start.3
  152.2 0.0 copy-start.2
  152.2 6.8 %all-to-all-start = ((bf16[28,112,64,32]{1,3,0,2:T(8,128)(2,1)}), bf16[28,112,64,32]{1,3,0,2:T(8,128)(2,1)}, u32[]{:S(2)}, u32[]{:S(2)}) async-start(bf16[28,112,64,32]{1,3,0,2:T(8,128)(2,1)} %copy.14), calls=%async_computation | async-start | bytes 29360128 | tf_op jit(solution)/shard_map/all_to_all | solution.py:22
  159.0 0.0 copy-done.3
  159.0 0.1 dynamic_slice.3
  159.1 0.1 broadcast_add_fusion
  159.1 0.0 copy-done.2
  159.1 0.1 broadcast_subtract_fusion
  159.2 161.0 %all-to-all-done = bf16[28,112,64,32]{1,3,0,2:T(8,128)(2,1)} async-done(((bf16[28,112,64,32]{1,3,0,2:T(8,128)(2,1)}), bf16[28,112,64,32]{1,3,0,2:T(8,128)(2,1)}, u32[]{:S(2)}, u32[]{:S(2)}) %all-to-all-start) | async-done | bytes 12845088 | tf_op jit(solution)/shard_map/all_to_all | solution.py:22
  320.3 14.4 %copy.16 = bf16[4,28,112,16,32]{2,4,3,1,0:T(8,128)(2,1)} copy(bf16[4,28,112,16,32]{2,4,1,3,0:T(8,128)(2,1)} %bitcast.6) | data formatting | bytes 25690112 | tf_op jit(solution)/shard_map/all_to_all | solution.py:22
  334.7 27.3 %fusion.10 = f32[16,32,32,64]{3,2,1,0:T(8,128)} fusion(bf16[112,112,16,32]{1,3,2,0:T(8,128)(2,1)} %bitcast.29, bf16[112,64]{0,1:T(8,128)(2,1)S(1)} %copy-done, bf16[112,32]{0,1:T(8,128)(2,1)S(1)} %copy-done.1), kind=kOutput, calls=%fused_computation.10 | convolution fusion | flops 647757824 | bytes 17060864 | tf_op jit(solution)/shard_map/pjba,pi->jbai/dot_general | solution.py:24
  362.0 13.9 %fusion.9 = f32[16,64]{1,0:T(8,128)} fusion(f32[16,32,32,64]{3,2,1,0:T(8,128)} %fusion.10, f32[32]{0:T(128)S(1)} %copy-done.2, f32[16,32,64]{2,1,0:T(8,128)S(1)} %broadcast_subtract_fusion), kind=kLoop, calls=%fused_computation.9 | loop fusion | flops 6290432 | bytes 4329600 | tf_op jit(solution)/shard_map/reduce_sum | solution.py:11
Async XLA Ops:
  0.0 0.7 copy-start
  0.0 48.5 %copy-start.1 = (bf16[112,32]{0,1:T(8,128)(2,1)S(1)}, bf16[112,32]{0,1:T(8,128)(2,1)}, u32[]{:S(2)}) copy-start(bf16[112,32]{0,1:T(8,128)(2,1)} %param.7) | copy-start | bytes 21508
  152.2 6.8 %copy-start.3 = (f32[64]{0:T(128)S(1)}, f32[64]{0:T(128)}, u32[]{:S(2)}) copy-start(f32[64]{0:T(128)} %param.8) | copy-start | bytes 772
  152.2 6.9 %copy-start.2 = (f32[32]{0:T(128)S(1)}, f32[32]{0:T(128)}, u32[]{:S(2)}) copy-start(f32[32]{0:T(128)} %param.9) | copy-start | bytes 388
  152.2 168.0 %all-to-all-start = ((bf16[28,112,64,32]{1,3,0,2:T(8,128)(2,1)}), bf16[28,112,64,32]{1,3,0,2:T(8,128)(2,1)}, u32[]{:S(2)}, u32[]{:S(2)}) async-start(bf16[28,112,64,32]{1,3,0,2:T(8,128)(2,1)} %copy.14), calls=%async_computation | async-start | bytes 29360128 | tf_op jit(solution)/shard_map/all_to_all | solution.py:22
where the time goes:
time: 379 us; the launch traced here: 376 us
  matrix products  164 us (43%)
  waiting for transfers between devices  161 us (42%)
  local copies, waits for them, and re-layouts  30.1 us (8%)
  other arithmetic  14 us (4%)
  starting transfers between devices  6.77 us (2%)
    all_to_all x1, waiting for transfers between devices, per_device(): half_mo = lax.all_to_all(half_mo, 'dev', 2, 0, tiled=True)  161 us
    dot_general x1, matrix products, per_device(): jnp.einsum('pqsj,sb->pqjb', t_one, c_vir, preferred_element_type=jnp.floa...  88.8 us
    dot_general x1, matrix products, per_device(): jnp.einsum('pqrs,rj->pqsj', a_ints, c_occ, preferred_element_type=jnp.flo...  47.8 us
    dot_general x1, matrix products, per_device(): jnp.einsum('pjba,pi->jbai', g_mat, c_occ, preferred_element_type=jnp.floa...  27.3 us
    convert_element_type x1, local copies, waits for them, and re-layouts, per_device(): jnp.einsum('pqsj,sb->pqjb', t_one, c_vir, preferred_element_type=jnp.floa...  14.9 us
    all_to_all x1, local copies, waits for them, and re-layouts, per_device(): half_mo = lax.all_to_all(half_mo, 'dev', 2, 0, tiled=True)  14.4 us
    reduce_sum x1, other arithmetic, pair_energies(): pair_ji = jnp.sum(v_mo * (2.0 * v_mo - v_swap) / denominator, axis=(1, 2))  13.9 us
  transfers between devices with their start and end apart: 1, of which 1 were waited for; matrix products, arithmetic and copies ran while one was open for 0% of the time, Pallas kernels for 0%

commit v1 on v0

v1 whole, which is shorter than its diff:
```python
import functools

import jax
import jax.numpy as jnp
from jax import lax
from jax.experimental import pallas as pl
from jax.experimental.pallas import tpu as pltpu
from jax.sharding import PartitionSpec as P

BF = jnp.bfloat16
F32 = jnp.float32
LANES = 128
GROUP_Q = 8
HALF_B = 16
PITCH = 40


def iota(shape, dim):
    return lax.broadcasted_iota(jnp.int32, shape, dim)


def dot32(a, b):
    return jnp.dot(a, b, preferred_element_type=F32)


def kernel(dims, eo_s, ev_s, eo_ref, cot_ref, cv_ref, a_hbm, out_ref,
           abuf, t0, t1, h0, h1, w2, w3, b4, gbuf, recv, vbuf, evc,
           a_sem, send_sem, recv_sem):
    rows, n, o, v, ndev = dims
    oj = o // ndev
    groups = n // GROUP_Q
    nb_hi = v // HALF_B
    half_cols = HALF_B * v
    me = lax.axis_index("dev")
    partner = me + 1 - 2 * (me % 2)
    peers = ((me + 2) % 4, (partner + 2) % 4, partner)

    def a_copy(p):
        slot = p % 3
        return pltpu.make_async_copy(a_hbm.at[p], abuf.at[slot], a_sem.at[slot])

    a_copy(0).start()
    a_copy(1).start()

    barrier = pltpu.get_barrier_semaphore()
    for d in peers:
        pl.semaphore_signal(barrier, inc=1, device_id={"dev": d},
                            device_id_type=pl.DeviceIdType.MESH)

    cv = cv_ref[...]
    col_b = (iota((v, 2 * LANES), 1) // LANES) * HALF_B + iota((v, 2 * LANES), 1) % HALF_B
    cvt = dot32(cv, jnp.where(iota((v, 2 * LANES), 0) == col_b, 1.0, 0.0).astype(BF))
    lane_q = (iota((n, 2 * LANES), 1) % LANES) // HALF_B
    w2[...] = jnp.zeros_like(w2)
    for q8 in range(GROUP_Q):
        w2[q8 * LANES:q8 * LANES + n, :] = jnp.where(lane_q == q8, cvt, 0.0).astype(BF)
    cv3 = dot32(cv, jnp.where(iota((v, half_cols), 0) == iota((v, half_cols), 1) % v, 1.0, 0.0).astype(BF)).astype(BF)
    chunk = 16 * 16
    mask3 = (iota((chunk, half_cols), 0) % HALF_B) == (iota((chunk, half_cols), 1) // v)

    def row_sel(c):
        return jnp.where(iota((chunk, n), 0) // 16 + 16 * c == iota((chunk, n), 1), 1.0, 0.0).astype(BF)

    for c in range(n // 16):
        w3[c * chunk:(c + 1) * chunk, :] = jnp.where(mask3, dot32(row_sel(c), cv3), 0.0).astype(BF)

    for a in range(v):
        evc[a:a + 1, :] = jnp.full((1, LANES), ev_s[a], F32)

    cot = cot_ref[...]
    pad = jnp.zeros((n, LANES - n), BF)

    def step1(p, t_ref, g_lo, g_hi):
        slot = p % 3
        for g in range(g_lo, g_hi):
            for k in range(GROUP_Q // 2):
                q = g * GROUP_Q + 2 * k
                w = jnp.concatenate([abuf[slot, q], pad, abuf[slot, q + 1], pad], axis=1)
                t_ref[g * o:(g + 1) * o, k * 2 * LANES:(k + 1) * 2 * LANES] = dot32(cot, w).astype(BF)

    def step2(t_ref, h_ref, g_lo, g_hi):
        res = dot32(t_ref[g_lo * o:g_hi * o, :], w2[...]).astype(BF)
        for g in range(g_lo, g_hi):
            for hi in range(nb_hi):
                h_ref[hi * o:(hi + 1) * o, g * LANES:(g + 1) * LANES] = (
                    res[(g - g_lo) * o:(g - g_lo + 1) * o, hi * LANES:(hi + 1) * LANES])

    def step3(p, h_ref):
        res = dot32(h_ref[...], w3[...]).astype(BF)
        for hi in range(nb_hi):
            for d in range(ndev):
                gbuf[p, d, :, hi * half_cols:(hi + 1) * half_cols] = (
                    res[hi * o + d * oj:hi * o + (d + 1) * oj, :])

    def send(p):
        for k, d in enumerate(peers):
            pltpu.make_async_remote_copy(
                src_ref=gbuf.at[p, d], dst_ref=recv.at[me * rows + p],
                send_sem=send_sem.at[k], recv_sem=recv_sem.at[k],
                device_id={"dev": d}, device_id_type=pl.DeviceIdType.MESH).start()
        recv[me * rows + p] = gbuf[p, me]

    tbufs, hbufs = (t0, t1), (h0, h1)
    cut = groups // 2

    def stage(t, par, s1=True, s2=True, s3=True, prefetch=True):
        if s1:
            a_copy(t).wait()
            if prefetch:
                a_copy(t + 2).start()
        for lo, hi in ((0, cut), (cut, groups)):
            if s1:
                step1(t, tbufs[par], lo, hi)
            if s2:
                step2(tbufs[1 - par], hbufs[1 - par], lo, hi)
        if s3:
            step3(t - 2, hbufs[par])

    stage(0, 0, s2=False, s3=False)
    stage(1, 1, s3=False)
    pl.semaphore_wait(barrier, 3)
    stage(2, 0)
    send(0)
    stage(3, 1)

    def pair(u, carry):
        t = 2 * u
        send(t - 3)
        stage(t, 0)
        send(t - 2)
        stage(t + 1, 1)
        return carry

    lax.fori_loop(2, rows // 2 - 1, pair, 0)
    send(rows - 5)
    stage(rows - 2, 0, prefetch=False)
    send(rows - 4)
    stage(rows - 1, 1, prefetch=False)
    send(rows - 3)
    stage(rows, 0, s1=False)
    send(rows - 2)
    stage(rows + 1, 1, s1=False, s2=False)
    send(rows - 1)

    lanes4 = oj * o
    cox = lax.dot_general(cot, jnp.where(iota((o, lanes4), 0) == iota((o, lanes4), 1) % o, 1.0, 0.0).astype(BF),
                          (((0,), (0,)), ((), ())), preferred_element_type=F32).astype(BF)
    mask4 = (iota((chunk, lanes4), 0) % 16) == (iota((chunk, lanes4), 1) // o)
    for c in range(n // 16):
        b4[c * chunk:(c + 1) * chunk, :] = jnp.where(mask4, dot32(row_sel(c), cox), 0.0).astype(BF)

    for k, d in enumerate(peers):
        whole = pltpu.make_async_remote_copy(
            src_ref=recv.at[pl.ds(me * rows, rows)], dst_ref=recv.at[pl.ds(d * rows, rows)],
            send_sem=send_sem.at[k], recv_sem=recv_sem.at[k],
            device_id={"dev": d}, device_id_type=pl.DeviceIdType.MESH)
        whole.wait_send()
        whole.wait_recv()

    g_all = recv.reshape(n * oj, v * v)
    b_per = 256 // v

    def step4(m, carry):
        cols = pl.ds(pl.multiple_of(m * 256, 256), 256)
        vm = lax.dot_general(g_all[:, cols], b4[...], (((0,), (0,)), ((), ())), preferred_element_type=F32)
        for b in range(b_per):
            base = pl.multiple_of((m * b_per + b) * PITCH, 8)
            for jt in range(lanes4 // LANES):
                vbuf[jt, pl.ds(base, v), :] = vm[b * v:(b + 1) * v, jt * LANES:(jt + 1) * LANES]
        return carry

    lax.fori_loop(0, v * v // 256, step4, 0)

    eo2 = jnp.concatenate([eo_ref[...], eo_ref[...]], axis=1)
    lane_lo = iota((1, LANES), 1) < o

    def step5(jt, carry):
        j0 = me * oj + 2 * jt
        eo_ji = jnp.where(lane_lo, eo_s[j0], eo_s[j0 + 1]) + eo2
        acc = jnp.zeros((8, LANES), F32)
        for b in range(v):
            eo_b = eo_ji - ev_s[b]
            for a in range(0, v, 8):
                x = vbuf[jt, b * PITCH + a:b * PITCH + a + 8, :]
                y = vbuf[jt, pl.ds(a * PITCH + b, 8, stride=PITCH), :]
                acc = acc + x * (2.0 * x - y) / (eo_b - evc[a:a + 8, :])
        tot = jnp.sum(acc, axis=0, keepdims=True)
        out_ref[pl.ds(2 * jt, 1), :] = tot[:, :o]
        out_ref[pl.ds(2 * jt + 1, 1), :] = tot[:, o:]
        return carry

    lax.fori_loop(0, lanes4 // LANES, step5, 0)


def solution(mesh):
    ndev = mesh.shape["dev"]

    def per_device(a_ints, c_occ, c_vir, eps_occ, eps_vir):
        rows, n = a_ints.shape[:2]
        o, v = c_occ.shape[1], c_vir.shape[1]
        oj = o // ndev
        vm = pl.BlockSpec(memory_space=pltpu.VMEM)
        sm = pl.BlockSpec(memory_space=pltpu.SMEM)
        e_t = pl.pallas_call(
            functools.partial(kernel, (rows, n, o, v, ndev)),
            out_shape=jax.ShapeDtypeStruct((oj, o), F32),
            in_specs=[sm, sm, vm, vm, vm, pl.BlockSpec(memory_space=pl.ANY)],
            out_specs=vm,
            scratch_shapes=[
                pltpu.VMEM((3, n, n, n), BF),
                pltpu.VMEM((n // GROUP_Q * o, GROUP_Q * LANES), BF),
                pltpu.VMEM((n // GROUP_Q * o, GROUP_Q * LANES), BF),
                pltpu.VMEM((v // HALF_B * o, n // GROUP_Q * LANES), BF),
                pltpu.VMEM((v // HALF_B * o, n // GROUP_Q * LANES), BF),
                pltpu.VMEM((GROUP_Q * LANES, 2 * LANES), BF),
                pltpu.VMEM((n * HALF_B, HALF_B * v), BF),
                pltpu.VMEM((n * oj, oj * o), BF),
                pltpu.VMEM((rows, ndev, oj, v * v), BF),
                pltpu.VMEM((n, oj, v * v), BF),
                pltpu.VMEM((oj * o // LANES, v * PITCH, LANES), F32),
                pltpu.VMEM((v, LANES), F32),
                pltpu.SemaphoreType.DMA((3,)),
                pltpu.SemaphoreType.DMA((3,)),
                pltpu.SemaphoreType.DMA((3,)),
            ],
            compiler_params=pltpu.CompilerParams(
                collective_id=0, has_side_effects=True, vmem_limit_bytes=60 * 2 ** 20),
            name="mp2",
        )(eps_occ, eps_vir, eps_occ[None, :], c_occ.T, c_vir, a_ints)
        return e_t.T

    return jax.shard_map(
        per_device,
        mesh=mesh,
        in_specs=(P(("frag", "dev")), P("frag"), P("frag"), P("frag"), P("frag")),
        out_specs=P("frag", "dev"),
        check_vma=False,
    )
```

time: 379 us -> 60 us (0.16)
  matrix products: 164 us -> 0 us
  waiting for transfers between devices: 161 us -> 0 us
  Pallas kernels: 0 us -> 57.1 us
  local copies, waits for them, and re-layouts: 30.1 us -> 2.69 us
  other arithmetic: 14 us -> 0 us
  starting transfers between devices: 6.77 us -> 0 us
    dot_general x3 -> x0, matrix products: 164 us -> none  [the longest x1 88.8 us: per_device(): jnp.einsum('pqsj,sb->pqjb', t_one, c_vir, preferred_element_type=jnp.floa...]
    all_to_all x1 -> x0, waiting for transfers between devices: 161 us -> none  [per_device(): half_mo = lax.all_to_all(half_mo, 'dev', 2, 0, tiled=True)]
    pallas_call x0 -> x1, Pallas kernels: none -> 57.1 us  [per_device(): pl.pallas_call(functools.partial(kernel, (rows, n, o, v, ndev)), out_shap...]
    convert_element_type x1 -> x0, local copies, waits for them, and re-layouts: 14.9 us -> none  [per_device(): jnp.einsum('pqsj,sb->pqjb', t_one, c_vir, preferred_element_type=jnp.floa...]
    all_to_all x1 -> x0, local copies, waits for them, and re-layouts: 14.4 us -> none  [per_device(): half_mo = lax.all_to_all(half_mo, 'dev', 2, 0, tiled=True)]
    reduce_sum x1 -> x0, other arithmetic: 13.9 us -> none  [pair_energies(): pair_ji = jnp.sum(v_mo * (2.0 * v_mo - v_swap) / denominator, axis=(1, 2))]
    all_to_all x1 -> x0, starting transfers between devices: 6.77 us -> none  [per_device(): half_mo = lax.all_to_all(half_mo, 'dev', 2, 0, tiled=True)]
  transfers between devices with their start and end apart: 1 -> 0, of which waited for: 1 -> 0; matrix products, arithmetic and copies ran while one was open for 0% -> 0% of each run, Pallas kernels for 0% -> 0%
where the time goes in v1:
time: 60 us; the launch traced here: 59.8 us
  Pallas kernels  57.1 us (95%)
  local copies, waits for them, and re-layouts  2.69 us (4%)
    pallas_call x1, Pallas kernels, per_device(): pl.pallas_call(functools.partial(kernel, (rows, n, o, v, ndev)), out_shap...  57.1 us
    unnamed x2, local copies, waits for them, and re-layouts  2.69 us

profile of v1, /device:TPU:0, one launch (start us, length us, event | category | flops | bytes accessed | tf_op | source)
XLA Modules:
  0.0 59.8 jit_solution(8539375061556791306)
XLA Ops:
  0.0 1.4 %copy.6.cv_ref = bf16[112,32]{1,0:T(8,128)(2,1)} copy(bf16[112,32]{0,1:T(8,128)(2,1)} %param.7) | data formatting | bytes 14336 | tf_op args[2]
  1.4 57.1 %mp2.1 = f32[16,64]{1,0:T(8,128)} custom-call(f32[64]{0:T(128)} %eo_s.1, f32[32]{0:T(128)} %ev_s.1, f32[1,64]{1,0:T(1,128)} %bitcast.5, bf16[64,112]{1,0:T(8,128)(2,1)} %bitcast.4, bf16[112,32]{1,0:T(8,128)(2,1)} %copy.6.cv_ref, bf16[28,112,112,112]{3,2,1,0:T(8,128)(2,1)} %a_hbm.1), custom_call_target="tpu_custom_call" | custom-call | tf_op jit(solution)/shard_map/mp2/pallas_call | solution.py:204
  58.5 1.3 %copy.8 = f32[64,16]{0,1:T(8,128)} copy(f32[64,16]{0,1:T(8,128)} %bitcast.3) | data formatting | bytes 8192

commit v2 on v1

v2 whole, which is shorter than its diff:
```python
import functools

import jax
import jax.numpy as jnp
from jax import lax
from jax.experimental import pallas as pl
from jax.experimental.pallas import tpu as pltpu
from jax.sharding import PartitionSpec as P

BF = jnp.bfloat16
F32 = jnp.float32
LANES = 128
GROUP_Q = 8
HALF_B = 16
PITCH = 40
LATE = 4


def iota(shape, dim):
    return lax.broadcasted_iota(jnp.int32, shape, dim)


def dot32(a, b):
    return jnp.dot(a, b, preferred_element_type=F32)


def dot_t(a, b):
    return lax.dot_general(a, b, (((0,), (0,)), ((), ())), preferred_element_type=F32)


def kernel(dims, eo_s, ev_s, eo_ref, cot_ref, cvt_ref, a_hbm, out_ref,
           abuf, t0, t1, h0, h1, w2, w3, b4, gbuf, recv, gt, vbuf, evc,
           a_sem, send_sem, recv_sem):
    rows, n, o, v, ndev = dims
    oj = o // ndev
    groups = n // GROUP_Q
    nb_hi = v // HALF_B
    half_cols = HALF_B * v
    early = rows - LATE
    me = lax.axis_index("dev")
    partner = me + 1 - 2 * (me % 2)
    peers = ((me + 2) % 4, (partner + 2) % 4, partner)

    def a_copy(p):
        slot = p % 3
        return pltpu.make_async_copy(a_hbm.at[p], abuf.at[slot], a_sem.at[slot])

    a_copy(0).start()
    a_copy(1).start()

    barrier = pltpu.get_barrier_semaphore()
    for d in peers:
        pl.semaphore_signal(barrier, inc=1, device_id={"dev": d},
                            device_id_type=pl.DeviceIdType.MESH)

    cvt = cvt_ref[...]
    col_b = (iota((v, 2 * LANES), 1) // LANES) * HALF_B + iota((v, 2 * LANES), 1) % HALF_B
    cv2 = dot_t(cvt, jnp.where(iota((v, 2 * LANES), 0) == col_b, 1.0, 0.0).astype(BF))
    lane_q = (iota((n, 2 * LANES), 1) % LANES) // HALF_B
    w2[...] = jnp.zeros_like(w2)
    for q8 in range(GROUP_Q):
        w2[q8 * LANES:q8 * LANES + n, :] = jnp.where(lane_q == q8, cv2, 0.0).astype(BF)
    cv3 = dot_t(cvt, jnp.where(iota((v, half_cols), 0) == iota((v, half_cols), 1) % v, 1.0, 0.0).astype(BF)).astype(BF)
    chunk = 16 * 16
    mask3 = (iota((chunk, half_cols), 0) % HALF_B) == (iota((chunk, half_cols), 1) // v)
    for c in range(n // 16):
        sel = jnp.where(iota((chunk, n), 0) // HALF_B + 16 * c == iota((chunk, n), 1), 1.0, 0.0).astype(BF)
        w3[c * chunk:(c + 1) * chunk, :] = jnp.where(mask3, dot32(sel, cv3), 0.0).astype(BF)

    cot = cot_ref[...]
    pad = jnp.zeros((n, LANES - n), BF)

    def step1(p, t_ref, g_lo, g_hi):
        slot = p % 3
        for g in range(g_lo, g_hi):
            for k in range(GROUP_Q // 2):
                q = g * GROUP_Q + 2 * k
                w = jnp.concatenate([abuf[slot, q], pad, abuf[slot, q + 1], pad], axis=1)
                t_ref[g * o:(g + 1) * o, k * 2 * LANES:(k + 1) * 2 * LANES] = dot32(cot, w).astype(BF)

    def step2(t_ref, h_ref, g_lo, g_hi):
        res = dot32(t_ref[g_lo * o:g_hi * o, :], w2[...]).astype(BF)
        for g in range(g_lo, g_hi):
            for hi in range(nb_hi):
                h_ref[hi * o:(hi + 1) * o, g * LANES:(g + 1) * LANES] = (
                    res[(g - g_lo) * o:(g - g_lo + 1) * o, hi * LANES:(hi + 1) * LANES])

    def step3(p, h_ref):
        res = dot32(h_ref[...], w3[...]).astype(BF)
        for hi in range(nb_hi):
            for d in range(ndev):
                gbuf[p, d, :, hi * half_cols:(hi + 1) * half_cols] = (
                    res[hi * o + d * oj:hi * o + (d + 1) * oj, :])

    def send(p):
        for k, d in enumerate(peers):
            pltpu.make_async_remote_copy(
                src_ref=gbuf.at[p, d], dst_ref=recv.at[p, me],
                send_sem=send_sem.at[k], recv_sem=recv_sem.at[k, p // early],
                device_id={"dev": d}, device_id_type=pl.DeviceIdType.MESH).start()
        recv[p, me] = gbuf[p, me]

    tbufs, hbufs = (t0, t1), (h0, h1)
    cut = groups // 2
    halves = ((0, cut), (cut, groups))

    def stage(t, par, s1=True, s2=True, s3=True, out=True, prefetch=True):
        if s1:
            a_copy(t).wait()
            if prefetch:
                a_copy(t + 2).start()
        if out:
            send(t - 3)
        if s3:
            step3(t - 2, hbufs[par])
        for lo, hi in halves:
            if s1:
                step1(t, tbufs[par], lo, hi)
            if s2:
                step2(tbufs[1 - par], hbufs[1 - par], lo, hi)

    stage(0, 0, s2=False, s3=False, out=False)
    step2(t0, h0, 0, groups)
    step3(0, h0)
    a_copy(1).wait()
    a_copy(3).start()
    step1(1, t1, 0, cut)
    pl.semaphore_wait(barrier, 3)
    send(0)
    step1(1, t1, cut, groups)
    stage(2, 0, s3=False, out=False)
    stage(3, 1, out=False)

    def pair(u, carry):
        t = 2 * u
        stage(t, 0)
        stage(t + 1, 1)
        return carry

    lax.fori_loop(2, rows // 2 - 1, pair, 0)
    stage(rows - 2, 0, prefetch=False)
    stage(rows - 1, 1, prefetch=False)
    stage(rows, 0, s1=False)
    send(rows - 2)
    step3(rows - 1, h1)

    for a in range(v):
        evc[a:a + 1, :] = jnp.full((1, LANES), ev_s[a], F32)

    lanes4 = oj * o
    cox = dot_t(cot, jnp.where(iota((o, lanes4), 0) == iota((o, lanes4), 1) % o, 1.0, 0.0).astype(BF)).astype(BF)
    mask4 = (iota((chunk, lanes4), 0) % oj) == (iota((chunk, lanes4), 1) // o)
    per = ndev * oj
    for c in range(n // 16):
        if c == 1:
            send(rows - 1)
        p_all = ((iota((chunk, n), 0) // oj) % ndev) * rows + (chunk // per) * c + iota((chunk, n), 0) // per
        sel = jnp.where(p_all == iota((chunk, n), 1), 1.0, 0.0).astype(BF)
        b4[c * chunk:(c + 1) * chunk, :] = jnp.where(mask4, dot32(sel, cox), 0.0).astype(BF)

    def arrived(lo, count, which):
        for k, d in enumerate(peers):
            pltpu.make_async_remote_copy(
                src_ref=gbuf.at[pl.ds(lo, count), d], dst_ref=recv.at[pl.ds(lo, count), d],
                send_sem=send_sem.at[k], recv_sem=recv_sem.at[k, which],
                device_id={"dev": d}, device_id_type=pl.DeviceIdType.MESH).wait_recv()

    arrived(0, early, 0)
    g_all = recv.reshape(n * oj, v * v)
    k_early = early * per
    b_per = 256 // v

    def step4(m, carry):
        cols = pl.ds(pl.multiple_of(m * 256, 256), 256)
        vm = dot_t(g_all[0:k_early, cols], b4[0:k_early, :])
        for b in range(b_per):
            base = pl.multiple_of((m * b_per + b) * PITCH, 8)
            for jt in range(lanes4 // LANES):
                vbuf[jt, pl.ds(base, v), :] = vm[b * v:(b + 1) * v, jt * LANES:(jt + 1) * LANES]
        return carry

    lax.fori_loop(0, v * v // 256, step4, 0)
    arrived(early, LATE, 1)
    gt[...] = g_all[k_early:, :].T

    def step4_late(nt):
        vm = dot32(gt[...], b4[k_early:, nt * 256:(nt + 1) * 256])
        for b in range(v):
            for h in range(2):
                vbuf[2 * nt + h, b * PITCH:b * PITCH + v, :] += (
                    vm[b * v:(b + 1) * v, h * LANES:(h + 1) * LANES])

    eo2 = jnp.concatenate([eo_ref[...], eo_ref[...]], axis=1)
    lane_lo = iota((1, LANES), 1) < o

    def step5(jt):
        j0 = me * oj + 2 * jt
        eo_ji = jnp.where(lane_lo, eo_s[j0], eo_s[j0 + 1]) + eo2
        diag = jnp.zeros((8, LANES), F32)
        off = jnp.zeros((8, LANES), F32)
        for b in range(v):
            eo_b = eo_ji - ev_s[b]
            for a in range(b // 8 * 8, v, 8):
                x = vbuf[jt, b * PITCH + a:b * PITCH + a + 8, :]
                y = vbuf[jt, pl.ds(a * PITCH + b, 8, stride=PITCH), :]
                den = eo_b - evc[a:a + 8, :]
                if a == b // 8 * 8:
                    diag = diag + x * (2.0 * x - y) / den
                else:
                    off = off + (x * (x - y) + y * y) / den
        tot = jnp.sum(diag + 2.0 * off, axis=0, keepdims=True)
        out_ref[2 * jt:2 * jt + 1, :] = tot[:, :o]
        out_ref[2 * jt + 1:2 * jt + 2, :] = tot[:, o:]

    blocks = lanes4 // 256
    step4_late(0)
    for nt in range(blocks):
        if nt + 1 < blocks:
            step4_late(nt + 1)
        step5(2 * nt)
        step5(2 * nt + 1)

    for k, d in enumerate(peers):
        pltpu.make_async_remote_copy(
            src_ref=gbuf.at[:, d], dst_ref=recv.at[:, d],
            send_sem=send_sem.at[k], recv_sem=recv_sem.at[k, 0],
            device_id={"dev": d}, device_id_type=pl.DeviceIdType.MESH).wait_send()


def solution(mesh):
    ndev = mesh.shape["dev"]

    def per_device(a_ints, c_occ, c_vir, eps_occ, eps_vir):
        rows, n = a_ints.shape[:2]
        o, v = c_occ.shape[1], c_vir.shape[1]
        oj = o // ndev
        vm = pl.BlockSpec(memory_space=pltpu.VMEM)
        sm = pl.BlockSpec(memory_space=pltpu.SMEM)
        e_t = pl.pallas_call(
            functools.partial(kernel, (rows, n, o, v, ndev)),
            out_shape=jax.ShapeDtypeStruct((oj, o), F32),
            in_specs=[sm, sm, vm, vm, vm, pl.BlockSpec(memory_space=pl.ANY)],
            out_specs=vm,
            scratch_shapes=[
                pltpu.VMEM((3, n, n, n), BF),
                pltpu.VMEM((n // GROUP_Q * o, GROUP_Q * LANES), BF),
                pltpu.VMEM((n // GROUP_Q * o, GROUP_Q * LANES), BF),
                pltpu.VMEM((v // HALF_B * o, n // GROUP_Q * LANES), BF),
                pltpu.VMEM((v // HALF_B * o, n // GROUP_Q * LANES), BF),
                pltpu.VMEM((GROUP_Q * LANES, 2 * LANES), BF),
                pltpu.VMEM((n * HALF_B, HALF_B * v), BF),
                pltpu.VMEM((n * oj, oj * o), BF),
                pltpu.VMEM((rows, ndev, oj, v * v), BF),
                pltpu.VMEM((rows, ndev, oj, v * v), BF),
                pltpu.VMEM((v * v, LATE * ndev * oj), BF),
                pltpu.VMEM((oj * o // LANES, v * PITCH, LANES), F32),
                pltpu.VMEM((v, LANES), F32),
                pltpu.SemaphoreType.DMA((3,)),
                pltpu.SemaphoreType.DMA((3,)),
                pltpu.SemaphoreType.DMA((3, 2)),
            ],
            compiler_params=pltpu.CompilerParams(
                collective_id=0, has_side_effects=True, vmem_limit_bytes=60 * 2 ** 20),
            name="mp2",
        )(eps_occ, eps_vir, eps_occ[None, :], c_occ.T, c_vir.T, a_ints)
        return e_t.T

    return jax.shard_map(
        per_device,
        mesh=mesh,
        in_specs=(P(("frag", "dev")), P("frag"), P("frag"), P("frag"), P("frag")),
        out_specs=P("frag", "dev"),
        check_vma=False,
    )
```

time: 60 us -> 54.4 us (0.907)
  Pallas kernels: 57.1 us -> 52.8 us
  local copies, waits for them, and re-layouts: 2.69 us -> 1.3 us
    pallas_call x1, Pallas kernels: 57.1 us -> 52.8 us  [per_device(): pl.pallas_call(functools.partial(kernel, (rows, n, o, v, ndev)), out_shap...]
    unnamed x2 -> x1, local copies, waits for them, and re-layouts: 2.69 us -> 1.3 us
where the time goes in v2:
time: 54.4 us; the launch traced here: 54.1 us
  Pallas kernels  52.8 us (97%)
  local copies, waits for them, and re-layouts  1.3 us (2%)
    pallas_call x1, Pallas kernels, per_device(): pl.pallas_call(functools.partial(kernel, (rows, n, o, v, ndev)), out_shap...  52.8 us
    unnamed x1, local copies, waits for them, and re-layouts  1.3 us

profile of v2, /device:TPU:0, one launch (start us, length us, event | category | flops | bytes accessed | tf_op | source)
XLA Modules:
  0.0 54.1 jit_solution(15197836045150299303)
XLA Ops:
  0.0 52.8 %mp2.1 = f32[16,64]{1,0:T(8,128)} custom-call(f32[64]{0:T(128)} %eo_s.1, f32[32]{0:T(128)} %ev_s.1, f32[1,64]{1,0:T(1,128)} %bitcast.7, bf16[64,112]{1,0:T(8,128)(2,1)} %bitcast.5, bf16[32,112]{1,0:T(8,128)(2,1)} %bitcast.6, bf16[28,112,112,112]{3,2,1,0:T(8,128)(2,1)} %a_hbm.1), custom_call_target="tpu_custom_call" | custom-call | tf_op jit(solution)/shard_map/mp2/pallas_call | solution.py:239
  52.9 1.3 %copy.7 = f32[64,16]{0,1:T(8,128)} copy(f32[64,16]{0,1:T(8,128)} %bitcast.4) | data formatting | bytes 8192

commit v3 on v2

v3 whole, which is shorter than its diff:
```python
import functools

import jax
import jax.numpy as jnp
from jax import lax
from jax.experimental import pallas as pl
from jax.experimental.pallas import tpu as pltpu
from jax.sharding import PartitionSpec as P

BF = jnp.bfloat16
F32 = jnp.float32
LANES = 128
GROUP_Q = 8
B_LOW = 8
PITCH = 40
SLOTS = 4
LATE = 4


def iota(shape, dim):
    return lax.broadcasted_iota(jnp.int32, shape, dim)


def dot32(a, b):
    return jnp.dot(a, b, preferred_element_type=F32)


def dot_t(a, b):
    return lax.dot_general(a, b, (((0,), (0,)), ((), ())), preferred_element_type=F32)


def kernel(dims, eo_hbm, ev_hbm, cot_hbm, cvt_hbm, a_hbm, out_ref,
           eo_ref, ev_ref, cot_ref, cvt_ref, abuf, tbuf, hbuf, w2, w3, b4, gbuf, recv, gt, vbuf, rtab, eoj, evc, coxb,
           in_sem, a0_sem, a_sem, send_sem, recv_sem):
    rows, n, o, v, ndev = dims
    oj = o // ndev
    groups = n // GROUP_Q
    nb_hi = v // B_LOW
    blk = GROUP_Q * B_LOW
    cols3 = B_LOW * v
    early = rows - LATE
    lanes4 = oj * o
    me = lax.axis_index("dev")
    partner = me + 1 - 2 * (me % 2)
    peers = ((me + 2) % 4, (partner + 2) % 4, partner)

    def a_copy(p):
        slot = p % SLOTS
        return pltpu.make_async_copy(a_hbm.at[p], abuf.at[slot], a_sem.at[slot])

    pieces = [(g, min(g + 4, groups)) for g in range(0, groups, 4)]
    first = [pltpu.make_async_copy(a_hbm.at[0, pl.ds(lo * GROUP_Q, (hi - lo) * GROUP_Q)],
                                   abuf.at[0, pl.ds(lo * GROUP_Q, (hi - lo) * GROUP_Q)], a0_sem.at[i])
             for i, (lo, hi) in enumerate(pieces)]
    small = [pltpu.make_async_copy(src, dst, in_sem.at[i]) for i, (src, dst) in enumerate(
        ((cvt_hbm, cvt_ref), (cot_hbm, cot_ref), (eo_hbm, eo_ref), (ev_hbm, ev_ref)))]
    small[0].start()
    small[1].start()
    for c in first:
        c.start()
    small[2].start()
    small[3].start()

    barrier = pltpu.get_barrier_semaphore()
    for d in peers:
        pl.semaphore_signal(barrier, inc=1, device_id={"dev": d},
                            device_id_type=pl.DeviceIdType.MESH)

    small[0].wait()
    small[1].wait()
    cvt = cvt_ref[...]
    lane2 = iota((v, 2 * LANES), 1)
    col_b = lane2 // blk * B_LOW + lane2 % B_LOW
    cv2 = dot_t(cvt, jnp.where(iota((v, 2 * LANES), 0) == col_b, 1.0, 0.0).astype(BF))
    lane_q = iota((n, 2 * LANES), 1) % blk // B_LOW
    w2[...] = jnp.zeros_like(w2)
    for q8 in range(GROUP_Q):
        w2[q8 * LANES:q8 * LANES + n, :] = jnp.where(lane_q == q8, cv2, 0.0).astype(BF)
    cv3 = dot_t(cvt, jnp.where(iota((v, cols3), 0) == iota((v, cols3), 1) % v, 1.0, 0.0).astype(BF)).astype(BF)
    chunk = 256
    mask3 = (iota((LANES, cols3), 0) % B_LOW) == (iota((LANES, cols3), 1) // v)
    per3 = LANES // B_LOW
    for c in range(n // per3):
        sel = jnp.where(iota((LANES, n), 0) // B_LOW + per3 * c == iota((LANES, n), 1), 1.0, 0.0).astype(BF)
        w3[c * LANES:(c + 1) * LANES, :] = jnp.where(mask3, dot32(sel, cv3), 0.0).astype(BF)

    cot = cot_ref[...]
    pad = jnp.zeros((n, LANES - n), BF)

    def step1(p, g_lo, g_hi):
        slot = p % SLOTS
        for g in range(g_lo, g_hi):
            for k in range(GROUP_Q // 2):
                q = g * GROUP_Q + 2 * k
                w = jnp.concatenate([abuf[slot, q], pad, abuf[slot, q + 1], pad], axis=1)
                tbuf[g * o:(g + 1) * o, k * 2 * LANES:(k + 1) * 2 * LANES] = dot32(cot, w).astype(BF)

    def step2(g_lo, g_hi):
        res = dot32(tbuf[g_lo * o:g_hi * o, :], w2[...]).astype(BF)
        for g in range(g_lo, g_hi, 2):
            at = (g - g_lo) * o
            for hi in range(nb_hi):
                hbuf[hi * o:(hi + 1) * o, g * blk:(g + 2) * blk] = jnp.concatenate(
                    [res[at:at + o, hi * blk:(hi + 1) * blk], res[at + o:at + 2 * o, hi * blk:(hi + 1) * blk]], axis=1)

    def step3(p):
        res = dot32(hbuf[...], w3[...]).astype(BF)
        for hi in range(nb_hi):
            for d in range(ndev):
                gbuf[p, d, :, hi * cols3:(hi + 1) * cols3] = (
                    res[hi * o + d * oj:hi * o + (d + 1) * oj, :])

    def send(p):
        for k, d in enumerate(peers):
            pltpu.make_async_remote_copy(
                src_ref=gbuf.at[p, d], dst_ref=recv.at[p, me],
                send_sem=send_sem.at[k], recv_sem=recv_sem.at[k, p // early],
                device_id={"dev": d}, device_id_type=pl.DeviceIdType.MESH).start()

    def keep(p):
        recv[p, me] = gbuf[p, me]

    mask4 = (iota((chunk, lanes4), 0) % oj) == (iota((chunk, lanes4), 1) // o)
    per = ndev * oj

    def operand4(c):
        p_all = ((iota((chunk, n), 0) // oj) % ndev) * rows + (chunk // per) * c + iota((chunk, n), 0) // per
        sel = jnp.where(p_all == iota((chunk, n), 1), 1.0, 0.0).astype(BF)
        at = pl.ds(pl.multiple_of(c * chunk, chunk), chunk)
        b4[at, :] = jnp.where(mask4, dot32(sel, coxb[...]), 0.0).astype(BF)

    def recips(b):
        ev_b = evc[pl.ds(b, 1), :]
        at = pl.ds(pl.multiple_of(b * v, v), v)
        for jt in range(lanes4 // LANES):
            rtab[jt, at, :] = 1.0 / ((eoj[jt:jt + 1, :] - ev_b) - evc[...])

    cut = groups // 2 + 1

    def stage(t, out=True, extra=None):
        if out:
            send(t - 2)
            keep(t - 2)
        a_copy(t).wait()
        ahead = t + 2
        if isinstance(t, int):
            if ahead < rows:
                a_copy(ahead).start()
        else:
            @pl.when(ahead < rows)
            def _():
                a_copy(ahead).start()
        step2(cut, groups)
        step1(t, 0, cut)
        step3(t - 1)
        if extra is not None:
            extra()
        step1(t, cut, groups)
        step2(0, cut)

    for i, (lo, hi) in enumerate(pieces):
        first[i].wait()
        if i in (0, 2):
            a_copy(1 + i // 2).start()
        step1(0, lo, hi)
        if i > 0:
            step2(*pieces[i - 1])
    step2(*pieces[-1])
    step3(0)
    a_copy(1).wait()
    a_copy(3).start()
    step1(1, 0, 2)
    pl.semaphore_wait(barrier, 3)
    send(0)
    keep(0)
    step1(1, 2, groups)
    step2(0, cut)

    small[2].wait()
    small[3].wait()
    eo = eo_ref[...]
    eo2 = jnp.concatenate([eo, eo], axis=1)
    for jt in range(lanes4 // LANES):
        j0 = me * oj + 2 * jt
        lo, hi = (jnp.sum(jnp.where(iota((1, o), 1) == j0 + h, eo, 0.0), axis=1, keepdims=True) for h in range(2))
        eoj[jt:jt + 1, :] = jnp.where(iota((1, LANES), 1) < o, lo, hi) + eo2
    ev_col = jnp.sum(jnp.where(iota((v, v), 0) == iota((v, v), 1), ev_ref[...], 0.0), axis=1, keepdims=True)
    evc[...] = jnp.broadcast_to(ev_col, (v, LANES))
    coxb[...] = dot_t(cot, jnp.where(iota((o, lanes4), 0) == iota((o, lanes4), 1) % o, 1.0, 0.0).astype(BF)).astype(BF)

    stage(2, out=False)
    lo5 = 3 + n // 16
    hi5 = lo5 + v // 2

    def with_operand4(t, carry):
        stage(t, extra=lambda: operand4(t - 3))
        return carry

    def with_recips(t, carry):
        def both():
            recips(2 * (t - lo5))
            recips(2 * (t - lo5) + 1)
        stage(t, extra=both)
        return carry

    lax.fori_loop(3, lo5, with_operand4, 0)
    lax.fori_loop(lo5, hi5, with_recips, 0)
    for t in range(hi5, rows):
        stage(t)
    send(rows - 2)
    keep(rows - 2)
    step2(cut, groups)
    step3(rows - 1)
    keep(rows - 1)

    def arrived(lo, count, which):
        for k, d in enumerate(peers):
            pltpu.make_async_remote_copy(
                src_ref=gbuf.at[pl.ds(lo, count), d], dst_ref=recv.at[pl.ds(lo, count), d],
                send_sem=send_sem.at[k], recv_sem=recv_sem.at[k, which],
                device_id={"dev": d}, device_id_type=pl.DeviceIdType.MESH).wait_recv()

    send(rows - 1)
    arrived(0, early, 0)
    g_all = recv.reshape(n * oj, v * v)
    k_early = early * per
    b_per = 256 // v

    def step4(m, carry):
        cols = pl.ds(pl.multiple_of(m * 256, 256), 256)
        vm = dot_t(g_all[0:k_early, cols], b4[0:k_early, :])
        for b in range(b_per):
            base = pl.multiple_of((m * b_per + b) * PITCH, 8)
            for jt in range(lanes4 // LANES):
                vbuf[jt, pl.ds(base, v), :] = vm[b * v:(b + 1) * v, jt * LANES:(jt + 1) * LANES]
        return carry

    lax.fori_loop(0, v * v // 256, step4, 0)
    arrived(early, LATE, 1)
    gt[...] = g_all[k_early:, :].T

    def step4_late(nt):
        vm = dot32(gt[...], b4[k_early:, nt * 256:(nt + 1) * 256])
        for b in range(v):
            for h in range(2):
                vbuf[2 * nt + h, b * PITCH:b * PITCH + v, :] += (
                    vm[b * v:(b + 1) * v, h * LANES:(h + 1) * LANES])

    def step5(jt):
        diag = jnp.zeros((8, LANES), F32)
        off = jnp.zeros((8, LANES), F32)
        for b in range(v):
            for a in range(b // 8 * 8, v, 8):
                x = vbuf[jt, b * PITCH + a:b * PITCH + a + 8, :]
                y = vbuf[jt, pl.ds(a * PITCH + b, 8, stride=PITCH), :]
                r = rtab[jt, b * v + a:b * v + a + 8, :]
                if a == b // 8 * 8:
                    diag = diag + x * (2.0 * x - y) * r
                else:
                    off = off + (x * (x - y) + y * y) * r
        tot = jnp.sum(diag + 2.0 * off, axis=0, keepdims=True)
        out_ref[2 * jt:2 * jt + 1, :] = tot[:, :o]
        out_ref[2 * jt + 1:2 * jt + 2, :] = tot[:, o:]

    blocks = lanes4 // 256
    step4_late(0)
    for nt in range(blocks):
        if nt + 1 < blocks:
            step4_late(nt + 1)
        step5(2 * nt)
        step5(2 * nt + 1)

    for k, d in enumerate(peers):
        pltpu.make_async_remote_copy(
            src_ref=gbuf.at[:, d], dst_ref=recv.at[:, d],
            send_sem=send_sem.at[k], recv_sem=recv_sem.at[k, 0],
            device_id={"dev": d}, device_id_type=pl.DeviceIdType.MESH).wait_send()


def solution(mesh):
    ndev = mesh.shape["dev"]

    def per_device(a_ints, c_occ, c_vir, eps_occ, eps_vir):
        rows, n = a_ints.shape[:2]
        o, v = c_occ.shape[1], c_vir.shape[1]
        oj = o // ndev
        hbm = pl.BlockSpec(memory_space=pl.ANY)
        lanes4 = oj * o
        e_t = pl.pallas_call(
            functools.partial(kernel, (rows, n, o, v, ndev)),
            out_shape=jax.ShapeDtypeStruct((oj, o), F32),
            in_specs=[hbm] * 5,
            out_specs=pl.BlockSpec(memory_space=pltpu.VMEM),
            scratch_shapes=[
                pltpu.VMEM((1, o), F32),
                pltpu.VMEM((1, v), F32),
                pltpu.VMEM((o, n), BF),
                pltpu.VMEM((v, n), BF),
                pltpu.VMEM((SLOTS, n, n, n), BF),
                pltpu.VMEM((n // GROUP_Q * o, GROUP_Q * LANES), BF),
                pltpu.VMEM((v // B_LOW * o, n * B_LOW), BF),
                pltpu.VMEM((GROUP_Q * LANES, 2 * LANES), BF),
                pltpu.VMEM((n * B_LOW, B_LOW * v), BF),
                pltpu.VMEM((n * oj, lanes4), BF),
                pltpu.VMEM((rows, ndev, oj, v * v), BF),
                pltpu.VMEM((rows, ndev, oj, v * v), BF),
                pltpu.VMEM((v * v, LATE * ndev * oj), BF),
                pltpu.VMEM((lanes4 // LANES, v * PITCH, LANES), F32),
                pltpu.VMEM((lanes4 // LANES, v * v, LANES), F32),
                pltpu.VMEM((lanes4 // LANES, LANES), F32),
                pltpu.VMEM((v, LANES), F32),
                pltpu.VMEM((n, lanes4), BF),
                pltpu.SemaphoreType.DMA((4,)),
                pltpu.SemaphoreType.DMA((4,)),
                pltpu.SemaphoreType.DMA((SLOTS,)),
                pltpu.SemaphoreType.DMA((3,)),
                pltpu.SemaphoreType.DMA((3, 2)),
            ],
            compiler_params=pltpu.CompilerParams(
                collective_id=0, has_side_effects=True, vmem_limit_bytes=62 * 2 ** 20),
            name="mp2",
        )(eps_occ[None, :], eps_vir[None, :], c_occ.T, c_vir.T, a_ints)
        return e_t.T

    return jax.shard_map(
        per_device,
        mesh=mesh,
        in_specs=(P(("frag", "dev")), P("frag"), P("frag"), P("frag"), P("frag")),
        out_specs=P("frag", "dev"),
        check_vma=False,
    )
```

time: 54.4 us -> 55.1 us (1.013)
  Pallas kernels: 52.8 us -> 53.5 us
    pallas_call x1, Pallas kernels: 52.8 us -> 53.5 us  [per_device(): pl.pallas_call(functools.partial(kernel, (rows, n, o, v, ndev)), out_shap...]
where the time goes in v3:
time: 55.1 us; the launch traced here: 54.8 us
  Pallas kernels  53.5 us (97%)
  local copies, waits for them, and re-layouts  1.3 us (2%)
    pallas_call x1, Pallas kernels, per_device(): pl.pallas_call(functools.partial(kernel, (rows, n, o, v, ndev)), out_shap...  53.5 us
    unnamed x1, local copies, waits for them, and re-layouts  1.3 us

profile of v3, /device:TPU:0, one launch (start us, length us, event | category | flops | bytes accessed | tf_op | source)
XLA Modules:
  0.0 54.8 jit_solution(2505968761840771521)
XLA Ops:
  0.0 53.5 %mp2.1 = f32[16,64]{1,0:T(8,128)} custom-call(f32[1,64]{1,0:T(1,128)} %bitcast.8, f32[1,32]{1,0:T(1,128)} %bitcast.9, bf16[64,112]{1,0:T(8,128)(2,1)} %bitcast.6, bf16[32,112]{1,0:T(8,128)(2,1)} %bitcast.7, bf16[28,112,112,112]{3,2,1,0:T(8,128)(2,1)} %a_hbm.1), custom_call_target="tpu_custom_call" | custom-call | tf_op jit(solution)/shard_map/mp2/pallas_call | solution.py:289
  53.6 1.3 %copy.7 = f32[64,16]{0,1:T(8,128)} copy(f32[64,16]{0,1:T(8,128)} %bitcast.5) | data formatting | bytes 8192

commit v4 on v3

--- a/solution.py
+++ b/solution.py
@@ -11,9 +11,8 @@
 F32 = jnp.float32
 LANES = 128
 GROUP_Q = 8
-B_LOW = 8
+HALF_B = 16
 PITCH = 40
-SLOTS = 4
 LATE = 4
 
 
@@ -35,9 +34,8 @@
     rows, n, o, v, ndev = dims
     oj = o // ndev
     groups = n // GROUP_Q
-    nb_hi = v // B_LOW
-    blk = GROUP_Q * B_LOW
-    cols3 = B_LOW * v
+    nb_hi = v // HALF_B
+    half_cols = HALF_B * v
     early = rows - LATE
     lanes4 = oj * o
     me = lax.axis_index("dev")
@@ -45,7 +43,7 @@
     peers = ((me + 2) % 4, (partner + 2) % 4, partner)
 
     def a_copy(p):
-        slot = p % SLOTS
+        slot = p % 3
         return pltpu.make_async_copy(a_hbm.at[p], abuf.at[slot], a_sem.at[slot])
 
     pieces = [(g, min(g + 4, groups)) for g in range(0, groups, 4)]
@@ -69,26 +67,24 @@
     small[0].wait()
     small[1].wait()
     cvt = cvt_ref[...]
-    lane2 = iota((v, 2 * LANES), 1)
-    col_b = lane2 // blk * B_LOW + lane2 % B_LOW
+    col_b = (iota((v, 2 * LANES), 1) // LANES) * HALF_B + iota((v, 2 * LANES), 1) % HALF_B
     cv2 = dot_t(cvt, jnp.where(iota((v, 2 * LANES), 0) == col_b, 1.0, 0.0).astype(BF))
-    lane_q = iota((n, 2 * LANES), 1) % blk // B_LOW
+    lane_q = (iota((n, 2 * LANES), 1) % LANES) // HALF_B
     w2[...] = jnp.zeros_like(w2)
     for q8 in range(GROUP_Q):
         w2[q8 * LANES:q8 * LANES + n, :] = jnp.where(lane_q == q8, cv2, 0.0).astype(BF)
-    cv3 = dot_t(cvt, jnp.where(iota((v, cols3), 0) == iota((v, cols3), 1) % v, 1.0, 0.0).astype(BF)).astype(BF)
-    chunk = 256
-    mask3 = (iota((LANES, cols3), 0) % B_LOW) == (iota((LANES, cols3), 1) // v)
-    per3 = LANES // B_LOW
-    for c in range(n // per3):
-        sel = jnp.where(iota((LANES, n), 0) // B_LOW + per3 * c == iota((LANES, n), 1), 1.0, 0.0).astype(BF)
-        w3[c * LANES:(c + 1) * LANES, :] = jnp.where(mask3, dot32(sel, cv3), 0.0).astype(BF)
+    cv3 = dot_t(cvt, jnp.where(iota((v, half_cols), 0) == iota((v, half_cols), 1) % v, 1.0, 0.0).astype(BF)).astype(BF)
+    chunk = 16 * 16
+    mask3 = (iota((chunk, half_cols), 0) % HALF_B) == (iota((chunk, half_cols), 1) // v)
+    for c in range(n // 16):
+        sel = jnp.where(iota((chunk, n), 0) // HALF_B + 16 * c == iota((chunk, n), 1), 1.0, 0.0).astype(BF)
+        w3[c * chunk:(c + 1) * chunk, :] = jnp.where(mask3, dot32(sel, cv3), 0.0).astype(BF)
 
     cot = cot_ref[...]
     pad = jnp.zeros((n, LANES - n), BF)
 
     def step1(p, g_lo, g_hi):
-        slot = p % SLOTS
+        slot = p % 3
         for g in range(g_lo, g_hi):
             for k in range(GROUP_Q // 2):
                 q = g * GROUP_Q + 2 * k
@@ -97,17 +93,16 @@
 
     def step2(g_lo, g_hi):
         res = dot32(tbuf[g_lo * o:g_hi * o, :], w2[...]).astype(BF)
-        for g in range(g_lo, g_hi, 2):
-            at = (g - g_lo) * o
+        for g in range(g_lo, g_hi):
             for hi in range(nb_hi):
-                hbuf[hi * o:(hi + 1) * o, g * blk:(g + 2) * blk] = jnp.concatenate(
-                    [res[at:at + o, hi * blk:(hi + 1) * blk], res[at + o:at + 2 * o, hi * blk:(hi + 1) * blk]], axis=1)
+                hbuf[hi * o:(hi + 1) * o, g * LANES:(g + 1) * LANES] = (
+                    res[(g - g_lo) * o:(g - g_lo + 1) * o, hi * LANES:(hi + 1) * LANES])
 
     def step3(p):
         res = dot32(hbuf[...], w3[...]).astype(BF)
         for hi in range(nb_hi):
             for d in range(ndev):
-                gbuf[p, d, :, hi * cols3:(hi + 1) * cols3] = (
+                gbuf[p, d, :, hi * half_cols:(hi + 1) * half_cols] = (
                     res[hi * o + d * oj:hi * o + (d + 1) * oj, :])
 
     def send(p):
@@ -116,8 +111,6 @@
                 src_ref=gbuf.at[p, d], dst_ref=recv.at[p, me],
                 send_sem=send_sem.at[k], recv_sem=recv_sem.at[k, p // early],
                 device_id={"dev": d}, device_id_type=pl.DeviceIdType.MESH).start()
-
-    def keep(p):
         recv[p, me] = gbuf[p, me]
 
     mask4 = (iota((chunk, lanes4), 0) % oj) == (iota((chunk, lanes4), 1) // o)
@@ -135,28 +128,24 @@
         for jt in range(lanes4 // LANES):
             rtab[jt, at, :] = 1.0 / ((eoj[jt:jt + 1, :] - ev_b) - evc[...])
 
-    cut = groups // 2 + 1
-
-    def stage(t, out=True, extra=None):
+    cut = groups // 2
+
+    def stage(t, s1=True, out=True, prefetch=True, extra=None):
+        if s1:
+            a_copy(t).wait()
+            if prefetch:
+                a_copy(t + 2).start()
         if out:
             send(t - 2)
-            keep(t - 2)
-        a_copy(t).wait()
-        ahead = t + 2
-        if isinstance(t, int):
-            if ahead < rows:
-                a_copy(ahead).start()
-        else:
-            @pl.when(ahead < rows)
-            def _():
-                a_copy(ahead).start()
         step2(cut, groups)
-        step1(t, 0, cut)
+        if s1:
+            step1(t, 0, cut)
         step3(t - 1)
         if extra is not None:
             extra()
-        step1(t, cut, groups)
-        step2(0, cut)
+        if s1:
+            step2(0, cut)
+            step1(t, cut, groups)
 
     for i, (lo, hi) in enumerate(pieces):
         first[i].wait()
@@ -172,9 +161,9 @@
     step1(1, 0, 2)
     pl.semaphore_wait(barrier, 3)
     send(0)
-    keep(0)
-    step1(1, 2, groups)
+    step1(1, 2, cut)
     step2(0, cut)
+    step1(1, cut, groups)
 
     small[2].wait()
     small[3].wait()
@@ -189,8 +178,6 @@
     coxb[...] = dot_t(cot, jnp.where(iota((o, lanes4), 0) == iota((o, lanes4), 1) % o, 1.0, 0.0).astype(BF)).astype(BF)
 
     stage(2, out=False)
-    lo5 = 3 + n // 16
-    hi5 = lo5 + v // 2
 
     def with_operand4(t, carry):
         stage(t, extra=lambda: operand4(t - 3))
@@ -203,15 +190,13 @@
         stage(t, extra=both)
         return carry
 
+    lo5 = 3 + n // 16
+    hi5 = lo5 + v // 2
     lax.fori_loop(3, lo5, with_operand4, 0)
     lax.fori_loop(lo5, hi5, with_recips, 0)
     for t in range(hi5, rows):
-        stage(t)
-    send(rows - 2)
-    keep(rows - 2)
-    step2(cut, groups)
-    step3(rows - 1)
-    keep(rows - 1)
+        stage(t, prefetch=t + 2 < rows)
+    stage(rows, s1=False)
 
     def arrived(lo, count, which):
         for k, d in enumerate(peers):
@@ -296,11 +281,11 @@
                 pltpu.VMEM((1, v), F32),
                 pltpu.VMEM((o, n), BF),
                 pltpu.VMEM((v, n), BF),
-                pltpu.VMEM((SLOTS, n, n, n), BF),
+                pltpu.VMEM((3, n, n, n), BF),
                 pltpu.VMEM((n // GROUP_Q * o, GROUP_Q * LANES), BF),
-                pltpu.VMEM((v // B_LOW * o, n * B_LOW), BF),
+                pltpu.VMEM((v // HALF_B * o, n // GROUP_Q * LANES), BF),
                 pltpu.VMEM((GROUP_Q * LANES, 2 * LANES), BF),
-                pltpu.VMEM((n * B_LOW, B_LOW * v), BF),
+                pltpu.VMEM((n * HALF_B, HALF_B * v), BF),
                 pltpu.VMEM((n * oj, lanes4), BF),
                 pltpu.VMEM((rows, ndev, oj, v * v), BF),
                 pltpu.VMEM((rows, ndev, oj, v * v), BF),
@@ -312,12 +297,12 @@
                 pltpu.VMEM((n, lanes4), BF),
                 pltpu.SemaphoreType.DMA((4,)),
                 pltpu.SemaphoreType.DMA((4,)),
-                pltpu.SemaphoreType.DMA((SLOTS,)),
+                pltpu.SemaphoreType.DMA((3,)),
                 pltpu.SemaphoreType.DMA((3,)),
                 pltpu.SemaphoreType.DMA((3, 2)),
             ],
             compiler_params=pltpu.CompilerParams(
-                collective_id=0, has_side_effects=True, vmem_limit_bytes=62 * 2 ** 20),
+                collective_id=0, has_side_effects=True, vmem_limit_bytes=60 * 2 ** 20),
             name="mp2",
         )(eps_occ[None, :], eps_vir[None, :], c_occ.T, c_vir.T, a_ints)
         return e_t.T

time: 55.1 us -> 53.6 us (0.973)
  Pallas kernels: 53.5 us -> 52 us
    pallas_call x1, Pallas kernels: 53.5 us -> 52 us  [per_device(): pl.pallas_call(functools.partial(kernel, (rows, n, o, v, ndev)), out_shap...]
where the time goes in v4:
time: 53.6 us; the launch traced here: 53.4 us
  Pallas kernels  52 us (97%)
  local copies, waits for them, and re-layouts  1.3 us (2%)
    pallas_call x1, Pallas kernels, per_device(): pl.pallas_call(functools.partial(kernel, (rows, n, o, v, ndev)), out_shap...  52 us
    unnamed x1, local copies, waits for them, and re-layouts  1.3 us

profile of v4, /device:TPU:0, one launch (start us, length us, event | category | flops | bytes accessed | tf_op | source)
XLA Modules:
  0.0 53.4 jit_solution(6598918725699917367)
XLA Ops:
  0.0 52.0 %mp2.1 = f32[16,64]{1,0:T(8,128)} custom-call(f32[1,64]{1,0:T(1,128)} %bitcast.8, f32[1,32]{1,0:T(1,128)} %bitcast.9, bf16[64,112]{1,0:T(8,128)(2,1)} %bitcast.6, bf16[32,112]{1,0:T(8,128)(2,1)} %bitcast.7, bf16[28,112,112,112]{3,2,1,0:T(8,128)(2,1)} %a_hbm.1), custom_call_target="tpu_custom_call" | custom-call | tf_op jit(solution)/shard_map/mp2/pallas_call | solution.py:274
  52.1 1.3 %copy.7 = f32[64,16]{0,1:T(8,128)} copy(f32[64,16]{0,1:T(8,128)} %bitcast.5) | data formatting | bytes 8192
